TPU v7x, 256 devices: a whole 4x4x8 slice. The times are simulated.
256 devices in a mesh: seq: 64 (over z_lo, x, y), tp: 4 (over z_hi, core).
Axes of the slice: x: 4, y: 4, z: 8 (z_hi: 2, z_lo: 4; z = z_hi * 4 + z_lo), core: 2. Of those that a mesh axis runs over, the one named last changes fastest.
Arguments:
- states: bfloat16 [64, 128, 2048], P('seq', None, 'tp'), may hold values from -60 to 60, as said below
- cotangent: bfloat16 [64, 128, 2048], P('seq', None, 'tp'), may hold values from -12 to 12, as said below
- wq: bfloat16 [2048, 2048], P(None, 'tp'), may hold values from -0.125 to 0.125
- wk: bfloat16 [2048, 512], P(None, 'tp'), may hold values from -0.125 to 0.125
- wv: bfloat16 [2048, 512], P(None, 'tp'), may hold values from -0.125 to 0.125
- wo: bfloat16 [2048, 2048], P('tp'), may hold values from -0.125 to 0.125
Outputs:
- gram: float32 [64, 64], P('seq')
Inputs may be any that keep to these rules, and one draw needn't show every extreme that they name: `states`: finite values. `cotangent`: finite values.
All inputs are finite; a program needn't handle non-finite values.
Results may differ from a plain program's by a relative error of at most 0.0025.
Values may be sent and summed in bfloat16 or wider, within the bound.
A program may use at most 64 MiB of HBM per device.

v0:
```python
import jax
import jax.numpy as jnp
from jax import lax
from jax.sharding import Mesh
from jax.sharding import PartitionSpec as P

HEADS = 32
KV_HEADS = 8
HEAD_DIM = 64
TP = ("tp_0", "tp_1")


theta_base = 500000.0


def from_behind(block, axis, distance):
    devices = range(lax.axis_size(axis))
    route = [((i - distance) % len(devices), i) for i in devices]
    return lax.ppermute(block, axis, route)


def cut_along(value, dim, size):
    before, after = (value.shape[:dim], value.shape[dim + 1 :])
    return jnp.moveaxis(value.reshape(*before, size, -1, *after), dim, 0)


def joined_along(blocks, dim):
    blocks = jnp.moveaxis(blocks, 0, dim)
    dims = blocks.shape
    return blocks.reshape(*dims[:dim], dims[dim] * dims[dim + 1], *dims[dim + 2 :])


def moved_by_axis(blocks, axes, order):
    dims = [lax.axis_size(a) for a in axes]
    blocks = blocks.reshape(*dims, *blocks.shape[1:])
    for k in order:
        blocks = lax.all_to_all(blocks, axes[k], split_axis=k, concat_axis=k, tiled=True)
    return blocks.reshape(-1, *blocks.shape[len(axes) :])


def exchange_by_chip(value, groups, order, split_dim, concat_dim):
    size = lax.axis_size(groups[0]) * lax.axis_size(groups[1])
    blocks = cut_along(value, split_dim, size)
    return joined_along(moved_by_axis(blocks, groups, order), concat_dim)


def copy_for_each(value, axis):
    size = lax.axis_size(axis)
    return lax.all_to_all(
        jnp.broadcast_to(value[None], (size, *value.shape)), axis, 0, 0, tiled=True
    )


def of_everyone(value, axis):
    everything = copy_for_each(value, axis)
    return jnp.sum(everything, axis=0)


def in_one(arrays, axis):
    ends = [0]
    for a in arrays:
        ends.append(ends[-1] + a.size)
    total = of_everyone(jnp.concatenate([a.ravel() for a in arrays]), axis)
    return tuple((total[b:e].reshape(a.shape) for a, b, e in zip(arrays, ends, ends[1:])))


def collect(value, axis, dim):
    blocks = copy_for_each(value, axis)
    return joined_along(blocks, dim)


def rope_tables(length, head_dim):
    half_dim = head_dim // 2
    freqs_k = theta_base ** (-(jnp.arange(half_dim, dtype=jnp.float32) * 2.0 / head_dim))
    angles = jnp.arange(length, dtype=jnp.float32)[:, None] * freqs_k[None, :]
    angles = jnp.concatenate([angles, angles], axis=1)
    return (jnp.cos(angles)[:, None, :], jnp.sin(angles)[:, None, :])


def rotate(values_in, cos_table, sine_table):
    half_dim = values_in.shape[-1] // 2
    turned = jnp.concatenate([-values_in[..., half_dim:], values_in[..., :half_dim]], axis=-1)
    return values_in * cos_table + turned * sine_table


def attention_factors(states, cotangent, wq, wk, wv, wo):
    seq_dev, length, part_width = states.shape
    full_states, full_cot = (
        lax.all_gather(states, TP, axis=2, tiled=True),
        lax.all_gather(cotangent, TP, axis=2, tiled=True),
    )
    model_width = full_states.shape[2]
    tok_rows = seq_dev * length
    kv_local = wk.shape[1] // HEAD_DIM
    group_size = HEADS // KV_HEADS
    cos_table, sine_table = rope_tables(length, HEAD_DIM)
    flat_states = full_states.reshape(tok_rows, model_width)
    query_heads = jnp.dot(flat_states, wq, preferred_element_type=jnp.float32).reshape(
        seq_dev, length, kv_local * group_size, HEAD_DIM
    )
    query_heads = (
        rotate(query_heads, cos_table, sine_table)
        .astype(jnp.bfloat16)
        .reshape(seq_dev, length, kv_local, group_size, HEAD_DIM)
    )
    key_heads = jnp.dot(flat_states, wk, preferred_element_type=jnp.float32).reshape(
        seq_dev, length, kv_local, HEAD_DIM
    )
    key_heads = rotate(key_heads, cos_table, sine_table).astype(jnp.bfloat16)
    value_heads = (
        jnp.dot(flat_states, wv, preferred_element_type=jnp.float32)
        .astype(jnp.bfloat16)
        .reshape(seq_dev, length, kv_local, HEAD_DIM)
    )
    scores = jnp.einsum(
        "sqkgd,stkd->skgqt", query_heads, key_heads, preferred_element_type=jnp.float32
    ) * HEAD_DIM ** (-0.5)
    causal = jnp.arange(length)[:, None] >= jnp.arange(length)[None, :]
    scores = jnp.where(causal, scores, -jnp.inf)
    weights_bf = jax.nn.softmax(scores, axis=-1).astype(jnp.bfloat16)
    attended = (
        jnp.einsum("skgqt,stkd->sqkgd", weights_bf, value_heads, preferred_element_type=jnp.float32)
        .astype(jnp.bfloat16)
        .reshape(tok_rows, part_width)
    )
    grad_attended = (
        lax.dot_general(
            full_cot.reshape(tok_rows, model_width),
            wo,
            (((1,), (1,)), ((), ())),
            preferred_element_type=jnp.float32,
        )
        .astype(jnp.bfloat16)
        .reshape(seq_dev, length, kv_local, group_size, HEAD_DIM)
    )
    value_gradient = (
        jnp.einsum(
            "skgqt,sqkgd->stkd", weights_bf, grad_attended, preferred_element_type=jnp.float32
        )
        .astype(jnp.bfloat16)
        .reshape(tok_rows, kv_local * HEAD_DIM)
    )
    return jnp.concatenate(
        [
            states.reshape(tok_rows, part_width),
            attended,
            cotangent.reshape(tok_rows, part_width),
            value_gradient,
        ],
        axis=1,
    )


def whole_tile(left_whole, right_whole, begin_col, end_col):
    return lax.dot_general(
        left_whole[:, :, begin_col:end_col],
        right_whole[:, :, begin_col:end_col],
        (((0, 2), (0, 2)), ((), ())),
        preferred_element_type=jnp.float32,
    )


def entire_block(own_whole, visitor_whole, part_width, seq_dev, length):
    full_width = own_whole.shape[2]
    states_tile = whole_tile(own_whole, visitor_whole, 0, part_width)
    attended_tile = whole_tile(own_whole, visitor_whole, part_width, 2 * part_width)
    cot_tile = whole_tile(own_whole, visitor_whole, 2 * part_width, 3 * part_width)
    values_tile = whole_tile(own_whole, visitor_whole, 3 * part_width, full_width)
    product = states_tile * values_tile + attended_tile * cot_tile
    return product.reshape(seq_dev, length, seq_dev, length).sum(axis=(1, 3))


def record(totals, block, distance, me_index, n_seq, half_rotation):
    row_acc, col_acc = totals
    seq_dev = block.shape[0]
    distance = jnp.asarray(distance, jnp.int32)
    offset = (me_index + distance) % n_seq * seq_dev
    zero_at = jnp.zeros((), jnp.int32)
    row_on = jnp.where(distance < half_rotation, 1.0, 0.0).astype(jnp.float32)
    row_acc = lax.dynamic_update_slice(row_acc, block * row_on, (zero_at, offset))
    mirror_on = jnp.where((distance > 0) & (distance <= half_rotation), 1.0, 0.0).astype(
        jnp.float32
    )
    col_acc = lax.dynamic_update_slice(col_acc, block.T * mirror_on, (offset, zero_at))
    return (row_acc, col_acc)


def on_device(states, cotangent, wq, wk, wv, wo):
    seq_dev, length, part_width = states.shape
    own_rows = attention_factors(states, cotangent, wq, wk, wv, wo)
    n_seq = lax.axis_size("seq")
    half_rotation = n_seq // 2
    me_index = lax.axis_index("seq")
    totals = (
        jnp.zeros((seq_dev, n_seq * seq_dev), jnp.float32),
        jnp.zeros((n_seq * seq_dev, seq_dev), jnp.float32),
    )
    n_tp = lax.axis_size(TP)
    tp_index = lax.axis_index(TP)
    own_whole = lax.all_gather(own_rows[None], TP, axis=0, tiled=True)
    shifted_parts = [own_rows] + [
        from_behind(own_rows, "seq", -offset) for offset in range(1, n_tp)
    ]
    visitor = exchange_by_chip(jnp.stack(shifted_parts), ("tp_0", "tp_1"), (1, 0), 0, 0)
    turn_count = half_rotation // n_tp + 1

    def measure_whole(totals_in, visitor_rows, distance):
        in_range = jnp.where(distance <= half_rotation, 1.0, 0.0).astype(jnp.float32)
        block = entire_block(own_whole, visitor_rows, part_width, seq_dev, length) * in_range
        return record(totals_in, block, distance, me_index, n_seq, half_rotation)

    totals = measure_whole(totals, visitor, tp_index)

    def stride_turn(step_index, carried):
        visitor_rows, totals_in = carried
        visitor_rows = from_behind(visitor_rows, "seq", -n_tp)
        return (
            visitor_rows,
            measure_whole(totals_in, visitor_rows, tp_index + (step_index + 1) * n_tp),
        )

    visitor, totals = lax.fori_loop(0, turn_count - 1, stride_turn, (visitor, totals))
    row_acc, col_acc = in_one((totals[0], totals[1]), TP)
    mirrored = lax.all_to_all(col_acc, "seq", split_axis=0, concat_axis=1, tiled=True)
    kernel = row_acc + mirrored
    own_block = lax.dynamic_slice_in_dim(kernel, me_index * seq_dev, seq_dev, 1)
    own_diag = jnp.diagonal(own_block)
    all_diag = collect(own_diag, "seq", 0)
    return kernel / jnp.sqrt(own_diag[:, None] * all_diag[None, :])


def solution(mesh):
    split = Mesh(mesh.devices.reshape(mesh.shape["seq"], 2, 2), ("seq", "tp_0", "tp_1"))
    placed = (
        P("seq", None, TP),
        P("seq", None, TP),
        P(None, TP),
        P(None, TP),
        P(None, TP),
        P(TP, None),
    )
    return jax.shard_map(
        on_device, mesh=split, in_specs=placed, out_specs=P("seq", None), check_vma=False
    )
```

profile of v0, /device:TPU:1, one launch (start us, length us, event | category | flops | bytes accessed | tf_op | source)
XLA Modules:
  0.0 601.5 jit_solution(8476827043644769787)
XLA Ops:
  6.6 14.6 %all_gather.9 = bf16[1,128,2048]{2,1,0:T(8,128)(2,1)S(1)} all-gather(bf16[1,128,512]{2,1,0:T(8,128)(2,1)} %param.8), channel_id=1, replica_groups=mesh['seq'=64,'tp_0'=2,'tp_1'=2] {'tp_0','tp_1'}, dimensions={2}, use_global_device_ids=true | all-gather | bytes 655360 | tf_op jit(solution)/shard_map/all_gather | solution.py:89
  24.3 11.3 %all_gather.10 = bf16[1,128,2048]{2,1,0:T(8,128)(2,1)S(1)} all-gather(bf16[1,128,512]{2,1,0:T(8,128)(2,1)S(1)} %copy-done.1), channel_id=1, replica_groups=mesh['seq'=64,'tp_0'=2,'tp_1'=2] {'tp_0','tp_1'}, dimensions={2}, use_global_device_ids=true | all-gather | bytes 655360 | tf_op jit(solution)/shard_map/all_gather | solution.py:90
  35.6 2.5 convolution_convert_fusion
  39.4 6.9 %collective-permute-start.1 = (bf16[128,1664]{1,0:T(8,128)(2,1)}, bf16[128,1664]{1,0:T(8,128)(2,1)S(1)}, u32[]{:S(2)}, u32[]{:S(2)}) collective-permute-start(bf16[128,1664]{1,0:T(8,128)(2,1)} %get-tuple-element.200), channel_id=1, source_target_pairs={{4,0},{8,4},{12,8},{16,12},{20,16},{24,20},{28,24},{32,28},{36,32}... | collective-permute-start | bytes 1277960 | tf_op jit(solution)/shard_map/ppermute | solution.py:19
  47.6 10.6 %collective-permute-done.1 = bf16[128,1664]{1,0:T(8,128)(2,1)S(1)} collective-permute-done((bf16[128,1664]{1,0:T(8,128)(2,1)}, bf16[128,1664]{1,0:T(8,128)(2,1)S(1)}, u32[]{:S(2)}, u32[]{:S(2)}) %collective-permute-start.1) | collective-permute-done | bytes 426016 | tf_op jit(solution)/shard_map/ppermute | solution.py:19
  58.2 25.2 %collective-permute-done.2 = bf16[128,1664]{1,0:T(8,128)(2,1)S(1)} collective-permute-done((bf16[128,1664]{1,0:T(8,128)(2,1)}, bf16[128,1664]{1,0:T(8,128)(2,1)S(1)}, u32[]{:S(2)}, u32[]{:S(2)}) %collective-permute-start.2) | collective-permute-done | bytes 426016 | tf_op jit(solution)/shard_map/ppermute | solution.py:19
  83.4 12.2 %collective-permute-done.3 = bf16[128,1664]{1,0:T(8,128)(2,1)S(1)} collective-permute-done((bf16[128,1664]{1,0:T(8,128)(2,1)}, bf16[128,1664]{1,0:T(8,128)(2,1)S(1)}, u32[]{:S(2)}, u32[]{:S(2)}) %collective-permute-start.3) | collective-permute-done | bytes 426016 | tf_op jit(solution)/shard_map/ppermute | solution.py:19
  96.0 5.7 all_to_all.38
  103.1 7.2 %all-to-all-start.1 = ((bf16[2,2,1,128,1664]{4,3,1,2,0:T(8,128)(2,1)}), bf16[2,2,1,128,1664]{4,3,1,2,0:T(8,128)(2,1)}, u32[]{:S(2)}, u32[]{:S(2)}) async-start(bf16[2,2,1,128,1664]{4,3,1,2,0:T(8,128)(2,1)} %copy.59), calls=%async_computation.1 | async-start | bytes 3407872 | tf_op jit(solution)/shard_map/all_to_all | solution.py:37
  110.3 24.3 %all-to-all-done.1 = bf16[2,2,1,128,1664]{4,3,1,2,0:T(8,128)(2,1)} async-done(((bf16[2,2,1,128,1664]{4,3,1,2,0:T(8,128)(2,1)}), bf16[2,2,1,128,1664]{4,3,1,2,0:T(8,128)(2,1)}, u32[]{:S(2)}, u32[]{:S(2)}) %all-to-all-start.1) | async-done | bytes 1703968 | tf_op jit(solution)/shard_map/all_to_all | solution.py:37
  138.8 2.2 fusion.18
  141.9 386.1 %while.19 = (s32[]{:T(128)}, bf16[4,128,1664]{2,1,0:T(8,128)(2,1)}, f32[1,64]{1,0:T(1,128)S(1)}, f32[64,1]{0,1:T(1,128)S(1)}, bf16[4,128,1664]{2,1,0:T(8,128)(2,...) while((s32[]{:T(128)}, bf16[4,128,1664]{2,1,0:T(8,128)(2,1)}, ...), condition=%wide.region_5.6_spmd, body=%wide.region_3.5_spmd.sunk | while | flops 218169344 | bytes 14025197 | solution.py:222
  142.1 37.0 %collective-permute-done = bf16[4,128,1664]{2,1,0:T(8,128)(2,1)} collective-permute-done((bf16[4,128,1664]{2,1,0:T(8,128)(2,1)}, bf16[4,128,1664]{2,1,0:T(8,128)(2,1)}, u32[]{:S(2)}, u32[]{:S(2)}) %collective-permute-start) | collective-permute-done | bytes 1703968 | tf_op jit(solution)/shard_map/while/body/eval_jaxpr/ppermute | solution.py:19
  183.2 2.2 fusion.78
  186.3 2.8 copy.81
  189.1 6.1 %collective-permute-start = (bf16[4,128,1664]{2,1,0:T(8,128)(2,1)}, bf16[4,128,1664]{2,1,0:T(8,128)(2,1)}, u32[]{:S(2)}, u32[]{:S(2)}) collective-permute-start(bf16[4,128,1664]{2,1,0:T(8,128)(2,1)} %get-tuple-element.268), channel_id=1, source_target_pairs={{16,0},{20,4},{24,8},{28,12},{32,16},{36,20},{40,24},{44,28},{48,3... | collective-permute-start | bytes 5111816 | tf_op jit(solution)/shard_map/while/body/eval_jaxpr/ppermute | solution.py:19
  195.2 26.5 %collective-permute-done = bf16[4,128,1664]{2,1,0:T(8,128)(2,1)} collective-permute-done((bf16[4,128,1664]{2,1,0:T(8,128)(2,1)}, bf16[4,128,1664]{2,1,0:T(8,128)(2,1)}, u32[]{:S(2)}, u32[]{:S(2)}) %collective-permute-start) | collective-permute-done | bytes 1703968 | tf_op jit(solution)/shard_map/while/body/eval_jaxpr/ppermute | solution.py:19
  225.9 2.2 fusion.78
  229.0 2.8 copy.81
  231.7 6.1 %collective-permute-start = (bf16[4,128,1664]{2,1,0:T(8,128)(2,1)}, bf16[4,128,1664]{2,1,0:T(8,128)(2,1)}, u32[]{:S(2)}, u32[]{:S(2)}) collective-permute-start(bf16[4,128,1664]{2,1,0:T(8,128)(2,1)} %get-tuple-element.268), channel_id=1, source_target_pairs={{16,0},{20,4},{24,8},{28,12},{32,16},{36,20},{40,24},{44,28},{48,3... | collective-permute-start | bytes 5111816 | tf_op jit(solution)/shard_map/while/body/eval_jaxpr/ppermute | solution.py:19
  237.8 25.7 %collective-permute-done = bf16[4,128,1664]{2,1,0:T(8,128)(2,1)} collective-permute-done((bf16[4,128,1664]{2,1,0:T(8,128)(2,1)}, bf16[4,128,1664]{2,1,0:T(8,128)(2,1)}, u32[]{:S(2)}, u32[]{:S(2)}) %collective-permute-start) | collective-permute-done | bytes 1703968 | tf_op jit(solution)/shard_map/while/body/eval_jaxpr/ppermute | solution.py:19
  267.7 2.2 fusion.78
  270.8 2.8 copy.81
  273.5 24.3 %collective-permute-start = (bf16[4,128,1664]{2,1,0:T(8,128)(2,1)}, bf16[4,128,1664]{2,1,0:T(8,128)(2,1)}, u32[]{:S(2)}, u32[]{:S(2)}) collective-permute-start(bf16[4,128,1664]{2,1,0:T(8,128)(2,1)} %get-tuple-element.268), channel_id=1, source_target_pairs={{16,0},{20,4},{24,8},{28,12},{32,16},{36,20},{40,24},{44,28},{48,3... | collective-permute-start | bytes 5111816 | tf_op jit(solution)/shard_map/while/body/eval_jaxpr/ppermute | solution.py:19
  297.9 36.0 %collective-permute-done = bf16[4,128,1664]{2,1,0:T(8,128)(2,1)} collective-permute-done((bf16[4,128,1664]{2,1,0:T(8,128)(2,1)}, bf16[4,128,1664]{2,1,0:T(8,128)(2,1)}, u32[]{:S(2)}, u32[]{:S(2)}) %collective-permute-start) | collective-permute-done | bytes 1703968 | tf_op jit(solution)/shard_map/while/body/eval_jaxpr/ppermute | solution.py:19
  338.0 2.2 fusion.78
  341.1 2.8 copy.81
  343.9 3.0 collective-permute-start
  346.8 33.5 %collective-permute-done = bf16[4,128,1664]{2,1,0:T(8,128)(2,1)} collective-permute-done((bf16[4,128,1664]{2,1,0:T(8,128)(2,1)}, bf16[4,128,1664]{2,1,0:T(8,128)(2,1)}, u32[]{:S(2)}, u32[]{:S(2)}) %collective-permute-start) | collective-permute-done | bytes 1703968 | tf_op jit(solution)/shard_map/while/body/eval_jaxpr/ppermute | solution.py:19
  384.5 2.2 fusion.78
  387.6 2.8 copy.81
  390.3 4.6 collective-permute-start
  395.0 31.1 %collective-permute-done = bf16[4,128,1664]{2,1,0:T(8,128)(2,1)} collective-permute-done((bf16[4,128,1664]{2,1,0:T(8,128)(2,1)}, bf16[4,128,1664]{2,1,0:T(8,128)(2,1)}, u32[]{:S(2)}, u32[]{:S(2)}) %collective-permute-start) | collective-permute-done | bytes 1703968 | tf_op jit(solution)/shard_map/while/body/eval_jaxpr/ppermute | solution.py:19
  430.3 2.2 fusion.78
  433.3 2.8 copy.81
  436.1 6.1 %collective-permute-start = (bf16[4,128,1664]{2,1,0:T(8,128)(2,1)}, bf16[4,128,1664]{2,1,0:T(8,128)(2,1)}, u32[]{:S(2)}, u32[]{:S(2)}) collective-permute-start(bf16[4,128,1664]{2,1,0:T(8,128)(2,1)} %get-tuple-element.268), channel_id=1, source_target_pairs={{16,0},{20,4},{24,8},{28,12},{32,16},{36,20},{40,24},{44,28},{48,3... | collective-permute-start | bytes 5111816 | tf_op jit(solution)/shard_map/while/body/eval_jaxpr/ppermute | solution.py:19
  442.2 30.3 %collective-permute-done = bf16[4,128,1664]{2,1,0:T(8,128)(2,1)} collective-permute-done((bf16[4,128,1664]{2,1,0:T(8,128)(2,1)}, bf16[4,128,1664]{2,1,0:T(8,128)(2,1)}, u32[]{:S(2)}, u32[]{:S(2)}) %collective-permute-start) | collective-permute-done | bytes 1703968 | tf_op jit(solution)/shard_map/while/body/eval_jaxpr/ppermute | solution.py:19
  475.2 1.5 fusion.77
  476.7 2.2 fusion.78
  479.8 2.8 copy.81
  482.5 6.1 %collective-permute-start = (bf16[4,128,1664]{2,1,0:T(8,128)(2,1)}, bf16[4,128,1664]{2,1,0:T(8,128)(2,1)}, u32[]{:S(2)}, u32[]{:S(2)}) collective-permute-start(bf16[4,128,1664]{2,1,0:T(8,128)(2,1)} %get-tuple-element.268), channel_id=1, source_target_pairs={{16,0},{20,4},{24,8},{28,12},{32,16},{36,20},{40,24},{44,28},{48,3... | collective-permute-start | bytes 5111816 | tf_op jit(solution)/shard_map/while/body/eval_jaxpr/ppermute | solution.py:19
  488.6 29.4 %collective-permute-done = bf16[4,128,1664]{2,1,0:T(8,128)(2,1)} collective-permute-done((bf16[4,128,1664]{2,1,0:T(8,128)(2,1)}, bf16[4,128,1664]{2,1,0:T(8,128)(2,1)}, u32[]{:S(2)}, u32[]{:S(2)}) %collective-permute-start) | collective-permute-done | bytes 1703968 | tf_op jit(solution)/shard_map/while/body/eval_jaxpr/ppermute | solution.py:19
  522.2 2.2 fusion.78
  525.3 2.8 copy.81
  528.2 18.4 %all_to_all.39 = f32[4,1,128]{2,1,0:T(1,128)S(1)} all-to-all(f32[4,1,128]{2,1,0:T(1,128)S(1)} %broadcast_in_dim.18), channel_id=1, replica_groups=mesh['seq'=64,'tp_0'=2,'tp_1'=2] {'tp_0','tp_1'}, dimensions={0} | all-to-all | bytes 4096 | tf_op jit(solution)/shard_map/all_to_all | solution.py:49
  547.3 22.0 %all-to-all-start.3 = ((f32[64,1,1]{2,1,0:T(1,128)}), f32[64,1,1]{2,1,0:T(1,128)S(1)}, u32[]{:S(2)}, u32[]{:S(2)}) async-start(f32[64,1,1]{2,1,0:T(1,128)} %copy.61), calls=%async_computation.3 | async-start | bytes 65536 | tf_op jit(solution)/shard_map/all_to_all | solution.py:224
  569.3 9.0 %all-to-all-done.3 = f32[64,1,1]{2,1,0:T(1,128)S(1)} async-done(((f32[64,1,1]{2,1,0:T(1,128)}), f32[64,1,1]{2,1,0:T(1,128)S(1)}, u32[]{:S(2)}, u32[]{:S(2)}) %all-to-all-start.3) | async-done | bytes 288 | tf_op jit(solution)/shard_map/all_to_all | solution.py:224
  580.1 12.8 %all_to_all.40 = f32[64,1,1]{2,1,0:T(1,128)S(1)} all-to-all(f32[64,1,1]{2,1,0:T(1,128)S(1)} %mul.237), channel_id=1, replica_groups=mesh['seq'=64,'tp_0'=2,'tp_1'=2] {'seq'}, dimensions={0} | all-to-all | bytes 512 | tf_op jit(solution)/shard_map/all_to_all | solution.py:49
  (94 shorter events, 49.7 us)
Async XLA Ops:
  6.5 14.7 %copy-start = (bf16[2048,512]{1,0:T(8,128)(2,1)S(1)}, bf16[2048,512]{1,0:T(8,128)(2,1)}, u32[]{:S(2)}) copy-start(bf16[2048,512]{1,0:T(8,128)(2,1)} %param.10) | copy-start | bytes 6291460
  6.5 128.1 %all-gather.3.cloned.1.call-start = ((), (), s32[]{:S(2)}) async-start(), calls=%async_computation.5 | async-start | bytes 2129920 | tf_op jit(solution)/shard_map/all_gather | solution.py:200
  21.2 1.0 copy-start.3
  22.6 1.0 copy-start.4
  23.1 1.2 copy-start.1
  35.6 2.9 copy-start.2
  39.4 18.8 %collective-permute-start.1 = (bf16[128,1664]{1,0:T(8,128)(2,1)}, bf16[128,1664]{1,0:T(8,128)(2,1)S(1)}, u32[]{:S(2)}, u32[]{:S(2)}) collective-permute-start(bf16[128,1664]{1,0:T(8,128)(2,1)} %get-tuple-element.200), channel_id=1, source_target_pairs={{4,0},{8,4},{12,8},{16,12},{20,16},{24,20},{28,24},{32,28},{36,32}... | collective-permute-start | bytes 1277960 | tf_op jit(solution)/shard_map/ppermute | solution.py:19
  46.3 37.1 %collective-permute-start.2 = (bf16[128,1664]{1,0:T(8,128)(2,1)}, bf16[128,1664]{1,0:T(8,128)(2,1)S(1)}, u32[]{:S(2)}, u32[]{:S(2)}) collective-permute-start(bf16[128,1664]{1,0:T(8,128)(2,1)} %get-tuple-element.200), channel_id=1, source_target_pairs={{8,0},{12,4},{16,8},{20,12},{24,16},{28,20},{32,24},{36,28},{40,32... | collective-permute-start | bytes 1277960 | tf_op jit(solution)/shard_map/ppermute | solution.py:19
  46.6 49.0 %collective-permute-start.3 = (bf16[128,1664]{1,0:T(8,128)(2,1)}, bf16[128,1664]{1,0:T(8,128)(2,1)S(1)}, u32[]{:S(2)}, u32[]{:S(2)}) collective-permute-start(bf16[128,1664]{1,0:T(8,128)(2,1)} %get-tuple-element.200), channel_id=1, source_target_pairs={{12,0},{16,4},{20,8},{24,12},{28,16},{32,20},{36,24},{40,28},{44,3... | collective-permute-start | bytes 1277960 | tf_op jit(solution)/shard_map/ppermute | solution.py:19
  103.1 31.5 %all-to-all-start.1 = ((bf16[2,2,1,128,1664]{4,3,1,2,0:T(8,128)(2,1)}), bf16[2,2,1,128,1664]{4,3,1,2,0:T(8,128)(2,1)}, u32[]{:S(2)}, u32[]{:S(2)}) async-start(bf16[2,2,1,128,1664]{4,3,1,2,0:T(8,128)(2,1)} %copy.59), calls=%async_computation.1 | async-start | bytes 3407872 | tf_op jit(solution)/shard_map/all_to_all | solution.py:37
  141.9 37.1 %collective-permute-start = (bf16[4,128,1664]{2,1,0:T(8,128)(2,1)}, bf16[4,128,1664]{2,1,0:T(8,128)(2,1)}, u32[]{:S(2)}, u32[]{:S(2)}) collective-permute-start(bf16[4,128,1664]{2,1,0:T(8,128)(2,1)} %get-tuple-element.268), channel_id=1, source_target_pairs={{16,0},{20,4},{24,8},{28,12},{32,16},{36,20},{40,24},{44,28},{48,3... | collective-permute-start | bytes 5111816 | tf_op jit(solution)/shard_map/while/body/eval_jaxpr/ppermute | solution.py:19
  189.1 32.6 %collective-permute-start = (bf16[4,128,1664]{2,1,0:T(8,128)(2,1)}, bf16[4,128,1664]{2,1,0:T(8,128)(2,1)}, u32[]{:S(2)}, u32[]{:S(2)}) collective-permute-start(bf16[4,128,1664]{2,1,0:T(8,128)(2,1)} %get-tuple-element.268), channel_id=1, source_target_pairs={{16,0},{20,4},{24,8},{28,12},{32,16},{36,20},{40,24},{44,28},{48,3... | collective-permute-start | bytes 5111816 | tf_op jit(solution)/shard_map/while/body/eval_jaxpr/ppermute | solution.py:19
  231.7 31.8 %collective-permute-start = (bf16[4,128,1664]{2,1,0:T(8,128)(2,1)}, bf16[4,128,1664]{2,1,0:T(8,128)(2,1)}, u32[]{:S(2)}, u32[]{:S(2)}) collective-permute-start(bf16[4,128,1664]{2,1,0:T(8,128)(2,1)} %get-tuple-element.268), channel_id=1, source_target_pairs={{16,0},{20,4},{24,8},{28,12},{32,16},{36,20},{40,24},{44,28},{48,3... | collective-permute-start | bytes 5111816 | tf_op jit(solution)/shard_map/while/body/eval_jaxpr/ppermute | solution.py:19
  273.5 60.3 %collective-permute-start = (bf16[4,128,1664]{2,1,0:T(8,128)(2,1)}, bf16[4,128,1664]{2,1,0:T(8,128)(2,1)}, u32[]{:S(2)}, u32[]{:S(2)}) collective-permute-start(bf16[4,128,1664]{2,1,0:T(8,128)(2,1)} %get-tuple-element.268), channel_id=1, source_target_pairs={{16,0},{20,4},{24,8},{28,12},{32,16},{36,20},{40,24},{44,28},{48,3... | collective-permute-start | bytes 5111816 | tf_op jit(solution)/shard_map/while/body/eval_jaxpr/ppermute | solution.py:19
  343.9 36.5 %collective-permute-start = (bf16[4,128,1664]{2,1,0:T(8,128)(2,1)}, bf16[4,128,1664]{2,1,0:T(8,128)(2,1)}, u32[]{:S(2)}, u32[]{:S(2)}) collective-permute-start(bf16[4,128,1664]{2,1,0:T(8,128)(2,1)} %get-tuple-element.268), channel_id=1, source_target_pairs={{16,0},{20,4},{24,8},{28,12},{32,16},{36,20},{40,24},{44,28},{48,3... | collective-permute-start | bytes 5111816 | tf_op jit(solution)/shard_map/while/body/eval_jaxpr/ppermute | solution.py:19
  390.3 35.7 %collective-permute-start = (bf16[4,128,1664]{2,1,0:T(8,128)(2,1)}, bf16[4,128,1664]{2,1,0:T(8,128)(2,1)}, u32[]{:S(2)}, u32[]{:S(2)}) collective-permute-start(bf16[4,128,1664]{2,1,0:T(8,128)(2,1)} %get-tuple-element.268), channel_id=1, source_target_pairs={{16,0},{20,4},{24,8},{28,12},{32,16},{36,20},{40,24},{44,28},{48,3... | collective-permute-start | bytes 5111816 | tf_op jit(solution)/shard_map/while/body/eval_jaxpr/ppermute | solution.py:19
  436.1 36.4 %collective-permute-start = (bf16[4,128,1664]{2,1,0:T(8,128)(2,1)}, bf16[4,128,1664]{2,1,0:T(8,128)(2,1)}, u32[]{:S(2)}, u32[]{:S(2)}) collective-permute-start(bf16[4,128,1664]{2,1,0:T(8,128)(2,1)} %get-tuple-element.268), channel_id=1, source_target_pairs={{16,0},{20,4},{24,8},{28,12},{32,16},{36,20},{40,24},{44,28},{48,3... | collective-permute-start | bytes 5111816 | tf_op jit(solution)/shard_map/while/body/eval_jaxpr/ppermute | solution.py:19
  482.5 35.5 %collective-permute-start = (bf16[4,128,1664]{2,1,0:T(8,128)(2,1)}, bf16[4,128,1664]{2,1,0:T(8,128)(2,1)}, u32[]{:S(2)}, u32[]{:S(2)}) collective-permute-start(bf16[4,128,1664]{2,1,0:T(8,128)(2,1)} %get-tuple-element.268), channel_id=1, source_target_pairs={{16,0},{20,4},{24,8},{28,12},{32,16},{36,20},{40,24},{44,28},{48,3... | collective-permute-start | bytes 5111816 | tf_op jit(solution)/shard_map/while/body/eval_jaxpr/ppermute | solution.py:19
  547.3 31.0 %all-to-all-start.3 = ((f32[64,1,1]{2,1,0:T(1,128)}), f32[64,1,1]{2,1,0:T(1,128)S(1)}, u32[]{:S(2)}, u32[]{:S(2)}) async-start(f32[64,1,1]{2,1,0:T(1,128)} %copy.61), calls=%async_computation.3 | async-start | bytes 65536 | tf_op jit(solution)/shard_map/all_to_all | solution.py:224
Sparse Core Ops, SparseCore 0:
  39.5 51.7 all-gather.2
where the time goes:
time: 604 us; the launch traced here: 602 us
  waiting for transfers between devices  331 us (55%)
  starting transfers between devices  93.8 us (16%)
  blocking collectives  62.9 us (10%)
  matrix products  61.7 us (10%)
  local copies, waits for them, and re-layouts  28.4 us (5%)
  between operations  14.3 us (2%)
    ppermute x11, waiting for transfers between devices, from_behind(): return lax.ppermute(block, axis, route)  298 us
    ppermute x11, starting transfers between devices, from_behind(): return lax.ppermute(block, axis, route)  64.6 us
    dot_general x36, matrix products, whole_tile(): lax.dot_general(left_whole[:, :, begin_col:end_col], right_whole[:, :, be...  57 us
    all_to_all x2, blocking collectives, copy_for_each(): lax.all_to_all(jnp.broadcast_to(value[None], (size, *value.shape)), axis,...  31.2 us
    all_to_all x1, waiting for transfers between devices, moved_by_axis(): lax.all_to_all(blocks, axes[k], split_axis=k, concat_axis=k, tiled=True)  24.3 us
    while x8, local copies, waits for them, and re-layouts  22.2 us
    all_to_all x1, starting transfers between devices, on_device(): lax.all_to_all(col_acc, 'seq', split_axis=0, concat_axis=1, tiled=True)  22 us
    all_gather x1, blocking collectives, attention_factors(): lax.all_gather(states, TP, axis=2, tiled=True)  14.6 us
  transfers between devices with their start and end apart: 14, of which 13 were waited for; matrix products, arithmetic and copies ran while one was open for 0% of the time, Pallas kernels for 0%

commit v1 on v0

v1 whole, which is shorter than its diff:
```python
import functools

import jax
import jax.numpy as jnp
import numpy as np
from jax import lax
from jax.experimental import pallas as pl
from jax.experimental.pallas import tpu as pltpu
from jax.sharding import Mesh
from jax.sharding import PartitionSpec as P

AXES = ("z", "x", "y", "h", "c")
MESH = pl.DeviceIdType.MESH
HEAD_DIM = 64
THETA = 500000.0
T = 128
PITCH = 72
BF = jnp.bfloat16
F32 = jnp.float32

PLANE = [(a, b) for a in range(4) for b in range(4) if (a, b) != (0, 0)]
COLUMN = [(w, c) for w in range(8) for c in range(2) if (w, c) != (0, 0)]


def nn(a, b):
    return lax.dot_general(a, b, (((1,), (0,)), ((), ())), preferred_element_type=F32)


def nt(a, b):
    return lax.dot_general(a, b, (((1,), (1,)), ((), ())), preferred_element_type=F32)


def rope_tables():
    k = np.arange(HEAD_DIM // 2, dtype=np.float64)
    freq = THETA ** (-2.0 * k / HEAD_DIM)
    angle = np.arange(T, dtype=np.float64)[:, None] * freq[None, :]
    cos, sin = np.cos(angle), np.sin(angle)
    cos = np.concatenate([cos, cos] * 2, axis=1)
    sin = np.concatenate([-sin, sin] * 2, axis=1)
    return cos.astype(np.float32), sin.astype(np.float32)


def rope(v, cos, sin):
    lane = lax.broadcasted_iota(jnp.int32, v.shape, 1)
    turned = jnp.where(lane % 64 < 32, pltpu.roll(v, 96, 1), pltpu.roll(v, 32, 1))
    return v * cos + turned * sin


def kernel(st, ct, wq, wk, wv, wo, cos, sin, out, wqb, wkb, wvb, wob, sbuf, cbuf, qacc, kacc, vacc,
           pst, a_own, v_own, abuf, vbuf, hsend, gsend, hbuf, gbuf, gram_in, kd, fin, f1, tbuf, f2,
           loc, tps, tpr, acs, acr, vcs, vcr, ccs, ccr, scs, scr, hs, hr, gs, gr, f1s, f1r, f2s, f2r):
    z, x, y, h, c = [lax.axis_index(a) for a in AXES]
    w = h * 4 + z
    p = h * 2 + c
    plane = x * 4 + y
    column = w * 2 + c
    other = 2 * (1 - h) + c

    def in_plane(a, b):
        return (z, (x + a) % 4, (y + b) % 4, h, c)

    def in_column(dw, dc):
        v = (w + dw) % 8
        return (v % 4, x, y, v // 4, (c + dc) % 2)

    sibling = in_column(0, 1)

    def remote(src, dst, send, recv, device):
        return pltpu.make_async_remote_copy(
            src_ref=src, dst_ref=dst, send_sem=send, recv_sem=recv, device_id=device, device_id_type=MESH)

    sent = []

    def push(src, dst, send, recv, device):
        copy = remote(src, dst, send, recv, device)
        copy.start()
        sent.append(copy)

    def arrived(slot, send, recv):
        remote(slot, slot, send, recv, sibling).wait_recv()

    loads = [pltpu.make_async_copy(a, b, loc.at[i]) for i, (a, b) in enumerate(
        [(st.at[0], sbuf.at[z, p]), (ct.at[0], cbuf.at[z, p]), (wq, wqb), (wk, wkb), (wv, wvb), (wo, wob)])]
    for load in loads:
        load.start()

    barrier = pltpu.get_barrier_semaphore()
    for a, b in PLANE:
        pl.semaphore_signal(barrier, inc=1, device_id=in_plane(a, b), device_id_type=MESH)
    for dw, dc in COLUMN:
        pl.semaphore_signal(barrier, inc=1, device_id=in_column(dw, dc), device_id_type=MESH)
    pl.semaphore_wait(barrier, len(PLANE) + len(COLUMN))

    loads[0].wait()
    push(sbuf.at[z, p], sbuf.at[z, p], tps.at[0], tpr.at[0], in_column(4, 0))
    push(sbuf.at[z, p], sbuf.at[z, p], tps.at[1], tpr.at[1], sibling)
    loads[1].wait()
    push(cbuf.at[z, p], cbuf.at[z, p], tps.at[2], tpr.at[2], in_column(4, 0))
    push(cbuf.at[z, p], cbuf.at[z, p], tps.at[3], tpr.at[3], sibling)

    def project(part, first):
        rows = pl.ds(pl.multiple_of(part * 512, 512), 512)
        s = sbuf[z, part]
        q, k, v = nn(s, wqb[rows, :]), nn(s, wkb[rows, :]), nn(s, wvb[rows, :])
        qacc[...] = q if first else qacc[...] + q
        kacc[...] = k if first else kacc[...] + k
        vacc[...] = v if first else vacc[...] + v

    for load in loads[2:5]:
        load.wait()
    project(p, True)
    arrived(sbuf.at[z, h * 2 + 1 - c], tps.at[1], tpr.at[1])
    project(h * 2 + 1 - c, False)
    arrived(sbuf.at[z, other], tps.at[0], tpr.at[0])
    push(sbuf.at[z, other], sbuf.at[z, other], tps.at[4], tpr.at[4], sibling)
    project(other, False)
    arrived(sbuf.at[z, 2 * (1 - h) + 1 - c], tps.at[4], tpr.at[4])
    project(2 * (1 - h) + 1 - c, False)

    cos_table, sin_table = cos[...], sin[...]
    lane = lax.broadcasted_iota(jnp.int32, (T, T), 1)
    key = rope(kacc[...], cos_table, sin_table)
    swapped = pltpu.roll(key, 64, 1)
    zero = jnp.zeros_like(key)
    low = lane < 64
    keys = [
        jnp.concatenate([jnp.where(low, key, zero), jnp.where(low, zero, swapped)], axis=0).astype(BF),
        jnp.concatenate([jnp.where(low, swapped, zero), jnp.where(low, zero, key)], axis=0).astype(BF),
    ]
    value_t = jnp.transpose(vacc[...]).astype(BF)
    row = lax.broadcasted_iota(jnp.int32, (T, T), 0)
    causal = row >= lane
    for j in range(4):
        query = rope(qacc[:, 128 * j : 128 * j + 128], cos_table, sin_table).astype(BF)
        scores = nt(query, keys[j // 2]) * HEAD_DIM ** (-0.5)
        for e in range(2):
            s = jnp.where(causal, scores[:, 128 * e : 128 * e + 128], -jnp.inf)
            s = jnp.exp(s - jnp.max(s, axis=1, keepdims=True))
            pst[2 * j + e] = (s / jnp.sum(s, axis=1, keepdims=True)).astype(BF)
    for g in range(2):
        probs = pst[4 * g : 4 * g + 4].reshape(4 * T, T)
        attended = nt(value_t[64 * g : 64 * g + 64], probs).astype(BF)
        for e in range(4):
            a_own[2 * g + e // 2, 64 * (e % 2) : 64 * (e % 2) + 64, :] = attended[:, 128 * e : 128 * e + 128]
    abuf[z, c] = a_own[z]
    push(abuf.at[z, c], abuf.at[z, c], acs.at[0], acr.at[0], sibling)
    for d in (1, 3, 2):
        to = (z + d) % 4
        push(a_own.at[to], abuf.at[z, c], acs.at[d], acr.at[d], (to, x, y, h, c))

    def gather(buf, send, recv):
        for i, (dw, parts) in enumerate([(1, (0, 1)), (7, (0, 1)), (2, (0,)), (6, (1,))]):
            for q in parts:
                part = 2 * q + c
                push(buf.at[z, part], buf.at[z, part], send.at[2 * i + q], recv.at[2 * i + q], in_column(dw, 0))

    def gathered(buf, send, recv, which):
        for i, back, parts in [(0, 3, (0, 1)), (1, 1, (0, 1)), (2, 2, (0,)), (3, 2, (1,))]:
            if back == which:
                for q in parts:
                    arrived(buf.at[(z + back) % 4, 2 * q + c], send.at[2 * i + q], recv.at[2 * i + q])

    arrived(cbuf.at[z, other], tps.at[2], tpr.at[2])
    push(cbuf.at[z, other], cbuf.at[z, other], tps.at[5], tpr.at[5], sibling)
    gather(cbuf, ccs, ccr)
    arrived(abuf.at[z, 1 - c], acs.at[0], acr.at[0])

    def forward_attended(d):
        came = (z - d) % 4
        arrived(abuf.at[came, c], acs.at[d], acr.at[d])
        push(abuf.at[came, c], abuf.at[came, c], acs.at[3 + d], acr.at[3 + d], sibling)

    def tiles(k, zz):
        left = abuf[zz].reshape(256, T)
        for q in range(2):
            block = nn(left, cbuf[zz, 2 * q + c]).astype(BF)
            for j in range(4):
                for e in range(2):
                    hsend[k, (4 * q + j) * 2 + e] = block[128 * e : 128 * e + 128, 128 * j : 128 * j + 128]
        hbuf[zz, plane] = hsend[k, plane]
        for i, (a, b) in enumerate(PLANE):
            to = (x + a) % 4 * 4 + (y + b) % 4
            push(hsend.at[k, to], hbuf.at[zz, plane], hs.at[k, i], hr.at[k, i], in_plane(a, b))

    tiles(0, z)

    loads[5].wait()
    arrived(cbuf.at[z, h * 2 + 1 - c], tps.at[3], tpr.at[3])
    arrived(cbuf.at[z, 2 * (1 - h) + 1 - c], tps.at[5], tpr.at[5])
    grad_t = nt(wob[:, 0:512], cbuf[z, 0])
    for part in range(1, 4):
        grad_t += nt(wob[:, 512 * part : 512 * part + 512], cbuf[z, part])
    grad_t = grad_t.astype(BF)
    for g in range(2):
        left = jnp.concatenate([grad_t[64 * (4 * g + e) : 64 * (4 * g + e) + 64] for e in range(4)], axis=1)
        gv = nn(left, pst[4 * g : 4 * g + 4].reshape(4 * T, T)).astype(BF)
        v_own[2 * g], v_own[2 * g + 1] = gv[0:32], gv[32:64]
    vbuf[z, c] = v_own[z]
    push(vbuf.at[z, c], vbuf.at[z, c], vcs.at[0], vcr.at[0], sibling)
    for d in (1, 3, 2):
        to = (z + d) % 4
        push(v_own.at[to], vbuf.at[z, c], vcs.at[d], vcr.at[d], (to, x, y, h, c))
    gather(sbuf, scs, scr)
    for d in (1, 3, 2):
        forward_attended(d)

    def settle(k, zz):
        def take(src, carry):
            gram_in[pl.ds(zz * 16 + src, 128, stride=PITCH), :] = hbuf[zz, src].astype(F32)
            return carry

        for i, (a, b) in enumerate(PLANE):
            src = (x - a) % 4 * 4 + (y - b) % 4
            arrived(hbuf.at[zz, src], hs.at[k, i], hr.at[k, i])
        lax.fori_loop(0, 16, take, 0)

    order = [0, 1, 3, 2]
    for k in range(1, 4):
        d = order[k]
        zz = (z + d) % 4
        arrived(abuf.at[zz, 1 - c], acs.at[3 + (4 - d) % 4], acr.at[3 + (4 - d) % 4])
        gathered(cbuf, ccs, ccr, d)
        tiles(k, zz)
        settle(k - 1, (z + order[k - 1]) % 4)

    for d in (1, 3, 2):
        came = (z - d) % 4
        arrived(vbuf.at[came, c], vcs.at[d], vcr.at[d])
        push(vbuf.at[came, c], vbuf.at[came, c], vcs.at[3 + d], vcr.at[3 + d], sibling)
    arrived(vbuf.at[z, 1 - c], vcs.at[0], vcr.at[0])
    for k in range(4):
        d = order[k]
        zz = (z + d) % 4
        if k > 0:
            arrived(vbuf.at[zz, 1 - c], vcs.at[3 + (4 - d) % 4], vcr.at[3 + (4 - d) % 4])
            gathered(sbuf, scs, scr, d)
        left = vbuf[zz].reshape(64, T)
        for q in range(2):
            block = nn(left, sbuf[zz, 2 * q + c]).astype(BF)
            for j in range(4):
                for e in range(2):
                    gsend[(4 * q + j) * 2 + e, zz] = block[32 * e : 32 * e + 32, 128 * j : 128 * j + 128]
    gbuf[plane] = gsend[plane]
    for i, (a, b) in enumerate(PLANE):
        to = (x + a) % 4 * 4 + (y + b) % 4
        push(gsend.at[to], gbuf.at[plane], gs.at[i], gr.at[i], in_plane(a, b))
    settle(3, (z + order[3]) % 4)
    for i, (a, b) in enumerate(PLANE):
        src = (x - a) % 4 * 4 + (y - b) % 4
        arrived(gbuf.at[src], gs.at[i], gr.at[i])

    def take_values(src, carry):
        for zz in range(4):
            gram_in[pl.ds(128 * PITCH + zz * 16 + src, 32, stride=PITCH), :] = gbuf[src, zz].astype(F32)
        return carry

    lax.fori_loop(0, 16, take_values, 0)

    def products(r, total):
        for u in range(4):
            at = pl.multiple_of((r * 8 + 2 * u) * PITCH, 8)
            both = jnp.concatenate([gram_in[pl.ds(at, 64), :], gram_in[pl.ds(at + PITCH, 64), :]], axis=1).astype(BF)
            total = total + nt(both, both)
        return total

    share = lax.fori_loop(0, 20, products, jnp.zeros((64, 64), F32))
    eye = lax.broadcasted_iota(jnp.int32, (64, 64), 0) == lax.broadcasted_iota(jnp.int32, (64, 64), 1)
    diag = jnp.sum(jnp.where(eye, share, 0.0), axis=0, keepdims=True)
    kd[...] = jnp.concatenate([share, jnp.broadcast_to(diag, (64, 64))], axis=1)
    for g in range(16):
        fin[g] = kd[pl.ds(g, 4, stride=16), :]
    f1[plane] = fin[plane]
    for i, (a, b) in enumerate(PLANE):
        to = (x + a) % 4 * 4 + (y + b) % 4
        push(fin.at[to], f1.at[plane], f1s.at[i], f1r.at[i], in_plane(a, b))
    for i, (a, b) in enumerate(PLANE):
        src = (x - a) % 4 * 4 + (y - b) % 4
        arrived(f1.at[src], f1s.at[i], f1r.at[i])
    rows = jnp.sum(f1[...], axis=0)
    for zz in range(4):
        tbuf[zz] = rows[zz : zz + 1]
    f2[column] = tbuf[z]
    for i, (dw, dc) in enumerate(COLUMN):
        to = in_column(dw, dc)
        push(tbuf.at[to[0]], f2.at[column], f2s.at[i], f2r.at[i], to)
    for i, (dw, dc) in enumerate(COLUMN):
        src = (w - dw) % 8 * 2 + (c - dc) % 2
        arrived(f2.at[src], f2s.at[i], f2r.at[i])
    total = jnp.sum(f2[...], axis=0)
    entries, diagonal = total[:, 0:64], total[:, 64:128]
    mine = lax.broadcasted_iota(jnp.int32, (1, 64), 1) == z * 16 + plane
    own = jnp.sum(jnp.where(mine, diagonal, 0.0), axis=1, keepdims=True)
    out[...] = entries / jnp.sqrt(own * diagonal)
    for copy in sent:
        copy.wait_send()


def on_device(states, cotangent, wq, wk, wv, wo):
    cos, sin = rope_tables()
    any_spec = pl.BlockSpec(memory_space=pl.ANY)
    vmem = pl.BlockSpec(memory_space=pltpu.VMEM)
    dma = pltpu.SemaphoreType.DMA
    shapes = [
        ((2048, 512), BF), ((2048, 128), BF), ((2048, 128), BF), ((512, 2048), BF),
        ((4, 4, T, 512), BF), ((4, 4, T, 512), BF),
        ((T, 512), F32), ((T, 128), F32), ((T, 128), F32),
        ((8, T, T), BF), ((4, 128, T), BF), ((4, 32, T), BF), ((4, 2, 128, T), BF), ((4, 2, 32, T), BF),
        ((4, 16, 128, 128), BF), ((16, 4, 32, 128), BF), ((4, 16, 128, 128), BF), ((16, 4, 32, 128), BF),
        ((160 * PITCH, 128), F32), ((64, 128), F32), ((16, 4, 128), F32), ((16, 4, 128), F32),
        ((4, 1, 128), F32), ((16, 1, 128), F32),
    ]
    sems = [(6,), (6,), (6,), (7,), (7,), (7,), (7,), (8,), (8,), (8,), (8,), (4, 15), (4, 15), (15,), (15,), (15,), (15,), (15,), (15,)]
    return pl.pallas_call(
        kernel,
        out_shape=jax.ShapeDtypeStruct((1, 64), F32),
        in_specs=[any_spec] * 6 + [vmem] * 2,
        out_specs=vmem,
        scratch_shapes=[pltpu.VMEM(s, t) for s, t in shapes] + [dma(s) for s in sems],
        compiler_params=pltpu.CompilerParams(
            collective_id=0, has_side_effects=True, vmem_limit_bytes=60 * 2**20),
        name="ntk_gram",
    )(states, cotangent, wq, wk, wv, wo, jnp.asarray(cos), jnp.asarray(sin))


def solution(mesh):
    split = Mesh(mesh.devices.reshape(4, 4, 4, 2, 2), AXES)
    seq, tp = ("z", "x", "y"), ("h", "c")
    return jax.shard_map(
        on_device,
        mesh=split,
        in_specs=(P(seq, None, tp), P(seq, None, tp), P(None, tp), P(None, tp), P(None, tp), P(tp, None)),
        out_specs=P(seq, None),
        check_vma=False,
    )
```

time: 604 us -> 81.3 us (0.13)
  waiting for transfers between devices: 331 us -> 0 us
  starting transfers between devices: 93.8 us -> 0 us
  Pallas kernels: 0 us -> 79.9 us
  blocking collectives: 62.9 us -> 0 us
  matrix products: 61.7 us -> 0 us
  local copies, waits for them, and re-layouts: 28.4 us -> 1.19 us
  between operations: 14.3 us -> 0.01 us
    ppermute x11 -> x0, waiting for transfers between devices: 298 us -> none  [from_behind(): return lax.ppermute(block, axis, route)]
    pallas_call x0 -> x1, Pallas kernels: none -> 79.9 us  [on_device(): pl.pallas_call(kernel, out_shape=jax.ShapeDtypeStruct((1, 64), F32), in_s...]
    ppermute x11 -> x0, starting transfers between devices: 64.6 us -> none  [from_behind(): return lax.ppermute(block, axis, route)]
    dot_general x43 -> x0, matrix products: 61.7 us -> none  [the longest x36 57 us: whole_tile(): lax.dot_general(left_whole[:, :, begin_col:end_col], right_whole[:, :, be...]
    all_to_all x3 -> x0, blocking collectives: 36.9 us -> none  [the longest x2 31.2 us: copy_for_each(): lax.all_to_all(jnp.broadcast_to(value[None], (size, *value.shape)), axis,...]
    all_to_all x2 -> x0, waiting for transfers between devices: 33.3 us -> none  [the longest x1 24.3 us: moved_by_axis(): lax.all_to_all(blocks, axes[k], split_axis=k, concat_axis=k, tiled=True)]
    all_to_all x2 -> x0, starting transfers between devices: 29.2 us -> none  [the longest x1 22 us: on_device(): lax.all_to_all(col_acc, 'seq', split_axis=0, concat_axis=1, tiled=True)]
    all_gather x2 -> x0, blocking collectives: 25.9 us -> none  [the longest x1 14.6 us: attention_factors(): lax.all_gather(states, TP, axis=2, tiled=True)]
  transfers between devices with their start and end apart: 14 -> 0, of which waited for: 13 -> 0; matrix products, arithmetic and copies ran while one was open for 0% -> 0% of each run, Pallas kernels for 0% -> 0%
where the time goes in v1:
time: 81.3 us; the launch traced here: 81.1 us
  Pallas kernels  79.9 us (98%)
  local copies, waits for them, and re-layouts  1.19 us (1%)
    pallas_call x1, Pallas kernels, on_device(): pl.pallas_call(kernel, out_shape=jax.ShapeDtypeStruct((1, 64), F32), in_s...  79.9 us

profile of v1, /device:TPU:1, one launch (start us, length us, event | category | flops | bytes accessed | tf_op | source)
XLA Modules:
  0.0 81.1 jit_solution(674304692206469319)
XLA Ops:
  0.0 79.9 %ntk_gram.1 = f32[1,64]{1,0:T(1,128)} custom-call(bf16[1,128,512]{2,1,0:T(8,128)(2,1)} %st.1, bf16[1,128,512]{2,1,0:T(8,128)(2,1)} %ct.1, bf16[2048,512]{1,0:T(8,128)(2,1)} %wq.1, bf16[2048,128]{1,0:T(8,128)(2,1)} %wk.1, bf16[2048,128]{1,0:T(8,128)(2,1)} %wv.1, bf16[512,2048]{1,0:T(8,128)(2,1)} %wo.1, f32[128,128]{1,0:T(8,128)} %constant.4.clone.cos, ...), custom_call_target="tpu_custom_call" | custom-call | tf_op jit(solution)/shard_map/ntk_gram/pallas_call | solution.py:313
  79.9 1.2 %copy.10 = f32[1,64]{1,0:T(1,128)} copy(f32[1,64]{1,0:T(1,128)} %ntk_gram.1) | data formatting | bytes 512

commit v2 on v1

v2 whole, which is shorter than its diff:
```python
import functools

import jax
import jax.numpy as jnp
import numpy as np
from jax import lax
from jax.experimental import pallas as pl
from jax.experimental.pallas import tpu as pltpu
from jax.sharding import Mesh
from jax.sharding import PartitionSpec as P

AXES = ("z", "x", "y", "h", "c")
MESH = pl.DeviceIdType.MESH
HEAD_DIM = 64
THETA = 500000.0
T = 128
PITCH = 72
BF = jnp.bfloat16
F32 = jnp.float32

PLANE = [(2, 2), (2, 1), (1, 2), (2, 3), (3, 2), (1, 1), (3, 3), (1, 3), (3, 1), (2, 0), (0, 2), (1, 0), (3, 0), (0, 1), (0, 3)]
COLUMN = [(w, c) for w in range(8) for c in range(2) if (w, c) != (0, 0)]


def nn(a, b):
    return lax.dot_general(a, b, (((1,), (0,)), ((), ())), preferred_element_type=F32)


def nt(a, b):
    return lax.dot_general(a, b, (((1,), (1,)), ((), ())), preferred_element_type=F32)


def rope_tables():
    k = np.arange(HEAD_DIM // 2, dtype=np.float64)
    freq = THETA ** (-2.0 * k / HEAD_DIM)
    angle = np.arange(T, dtype=np.float64)[:, None] * freq[None, :]
    cos, sin = np.cos(angle), np.sin(angle)
    cos = np.concatenate([cos, cos] * 2, axis=1)
    sin = np.concatenate([-sin, sin] * 2, axis=1)
    return cos.astype(np.float32), sin.astype(np.float32)


def rope(v, cos, sin):
    lane = lax.broadcasted_iota(jnp.int32, v.shape, 1)
    turned = jnp.where(lane % 64 < 32, pltpu.roll(v, 96, 1), pltpu.roll(v, 32, 1))
    return v * cos + turned * sin


def kernel(st, ct, wq, wk, wv, wo, cos_in, sin_in, out, wqb, wkb, wvb, wob, cos, sin, sbuf, cbuf, sq, cq, qacc, kacc, vacc,
           pst, abuf, vbuf, tsend, tbuf, gram_in, kd, fin, f1, rowbuf, f2,
           loc, tps, tpr, acs, acr, vcs, vcr, ccs, ccr, scs, scr, hs, hr, gs, gr, f1s, f1r, f2s, f2r):
    z, x, y, h, c = [lax.axis_index(a) for a in AXES]
    w = h * 4 + z
    p = h * 2 + c
    plane = x * 4 + y
    column = w * 2 + c

    def in_plane(a, b):
        return (z, (x + a) % 4, (y + b) % 4, h, c)

    def in_column(dw, dc):
        v = (w + dw) % 8
        return (v % 4, x, y, v // 4, (c + dc) % 2)

    sibling = in_column(0, 1)
    opposite = in_column(4, 0)

    def remote(src, dst, send, recv, device):
        return pltpu.make_async_remote_copy(
            src_ref=src, dst_ref=dst, send_sem=send, recv_sem=recv, device_id=device, device_id_type=MESH)

    sent = []

    def push(src, dst, send, recv, device):
        copy = remote(src, dst, send, recv, device)
        copy.start()
        sent.append(copy)

    def arrived(slot, send, recv):
        remote(slot, slot, send, recv, sibling).wait_recv()

    loads = [pltpu.make_async_copy(a, b, loc.at[i]) for i, (a, b) in enumerate(
        [(st.at[0], sbuf.at[p]), (ct.at[0], cbuf.at[p]), (wq, wqb), (wk, wkb), (wv, wvb), (cos_in, cos), (sin_in, sin), (wo, wob)])]
    for load in loads:
        load.start()

    barrier = pltpu.get_barrier_semaphore()
    for dw, dc in COLUMN:
        pl.semaphore_signal(barrier, inc=1, device_id=in_column(dw, dc), device_id_type=MESH)
    for a, b in PLANE:
        pl.semaphore_signal(barrier, inc=1, device_id=in_plane(a, b), device_id_type=MESH)
    pl.semaphore_wait(barrier, len(PLANE) + len(COLUMN))

    halves = [pl.ds(0, 256), pl.ds(256, 256)]

    def exchange(buf, base):
        for i, cols in enumerate(halves):
            push(buf.at[p, :, cols], buf.at[p, :, cols], tps.at[base + i], tpr.at[base + i], opposite)
        push(buf.at[p], buf.at[p], tps.at[base + 2], tpr.at[base + 2], sibling)

    def from_sibling(buf, base):
        arrived(buf.at[h * 2 + 1 - c], tps.at[base + 2], tpr.at[base + 2])

    def from_opposite(buf, base, i):
        part = buf.at[2 * (1 - h) + c, :, halves[i]]
        arrived(part, tps.at[base + i], tpr.at[base + i])
        push(part, part, tps.at[base + 3 + i], tpr.at[base + 3 + i], sibling)

    def forwarded(buf, base, i):
        arrived(buf.at[2 * (1 - h) + 1 - c, :, halves[i]], tps.at[base + 3 + i], tpr.at[base + 3 + i])

    loads[0].wait()
    exchange(sbuf, 0)
    loads[1].wait()
    exchange(cbuf, 5)
    def project(part, i, width, first=False):
        rows = pl.ds(pl.multiple_of(part * 512 + 256 * i, 256), width)
        s = sbuf[part, :, 256 * i : 256 * i + width]
        q, k, v = nn(s, wqb[rows, :]), nn(s, wkb[rows, :]), nn(s, wvb[rows, :])
        qacc[...] = q if first else qacc[...] + q
        kacc[...] = k if first else kacc[...] + k
        vacc[...] = v if first else vacc[...] + v

    for load in loads[2:7]:
        load.wait()
    project(p, 0, 512, True)
    from_sibling(sbuf, 0)
    project(h * 2 + 1 - c, 0, 512)
    cos_table, sin_table = cos[...], sin[...]
    for i in range(2):
        from_opposite(sbuf, 0, i)
        project(2 * (1 - h) + c, i, 256)
    for i in range(2):
        forwarded(sbuf, 0, i)
        project(2 * (1 - h) + 1 - c, i, 256)

    lane = lax.broadcasted_iota(jnp.int32, (T, T), 1)
    key = rope(kacc[...], cos_table, sin_table)
    swapped = pltpu.roll(key, 64, 1)
    zero = jnp.zeros_like(key)
    low = lane < 64
    keys = [
        jnp.concatenate([jnp.where(low, key, zero), jnp.where(low, zero, swapped)], axis=0).astype(BF),
        jnp.concatenate([jnp.where(low, swapped, zero), jnp.where(low, zero, key)], axis=0).astype(BF),
    ]
    value_t = jnp.transpose(vacc[...]).astype(BF)
    row = lax.broadcasted_iota(jnp.int32, (T, T), 0)
    causal = row >= lane
    for j in range(4):
        query = rope(qacc[:, 128 * j : 128 * j + 128], cos_table, sin_table).astype(BF)
        scores = nt(query, keys[j // 2]) * HEAD_DIM ** (-0.5)
        for e in range(2):
            s = jnp.where(causal, scores[:, 128 * e : 128 * e + 128], -jnp.inf)
            s = jnp.exp(s - jnp.max(s, axis=1, keepdims=True))
            pst[2 * j + e] = (s / jnp.sum(s, axis=1, keepdims=True)).astype(BF)
    for g in range(2):
        probs = pst[4 * g : 4 * g + 4].reshape(4 * T, T)
        attended = nt(value_t[64 * g : 64 * g + 64], probs).astype(BF)
        for e in range(4):
            r = 64 * (4 * g + e)
            abuf[z, r : r + 64, :] = attended[:, 128 * e : 128 * e + 128]

    def along_z(buf, send, recv, k):
        push(buf.at[z], buf.at[z], send.at[k], recv.at[k], (z ^ k, x, y, h, c))

    along_z(abuf, acs, acr, 1)

    mine = pl.ds(pl.multiple_of(64 * c, 64), 64)
    others = pl.ds(pl.multiple_of(64 * (1 - c), 64), 64)

    def quarter(buf, kept, send, recv, i, dw):
        push(buf.at[(z + dw) % 4, mine, :], kept.at[z, mine, :], send.at[i], recv.at[i], in_column(dw, 0))

    def relay(kept, send, recv, k):
        i = 2 if k == 2 else (1 - z % 2 if k == 1 else z % 2)
        arrived(kept.at[z ^ k, mine, :], send.at[i], recv.at[i])
        push(kept.at[z ^ k, mine, :], kept.at[z ^ k, mine, :], send.at[2 + k], recv.at[2 + k], sibling)

    def complete(kept, send, recv, k):
        arrived(kept.at[z ^ k, others, :], send.at[2 + k], recv.at[2 + k])

    from_sibling(cbuf, 5)
    from_opposite(cbuf, 5, 0)
    from_opposite(cbuf, 5, 1)
    forwarded(cbuf, 5, 0)
    forwarded(cbuf, 5, 1)
    quarter(cbuf, cq, ccs, ccr, 0, 1)
    quarter(cbuf, cq, ccs, ccr, 1, 7)
    quarter(cbuf, cq, ccs, ccr, 2, 6)
    along_z(abuf, acs, acr, 3)

    def tile_wo(k, right):
        for rb in range(4):
            block = nn(abuf[z ^ k, 128 * rb : 128 * rb + 128, :], right).astype(BF)
            for cb in range(4):
                tsend[k, rb * 4 + cb, 0:128, :] = block[:, 128 * cb : 128 * cb + 128]
        tbuf[z ^ k, plane, 0:128, :] = tsend[k, plane, 0:128, :]
        for i, (a, b) in enumerate(PLANE):
            to = (x + a) % 4 * 4 + (y + b) % 4
            push(tsend.at[k, to, pl.ds(0, 128)], tbuf.at[z ^ k, plane, pl.ds(0, 128)], hs.at[k, i], hr.at[k, i], in_plane(a, b))

    def tile_wv(k, right):
        block = nn(vbuf[z ^ k], right).astype(BF)
        for rb in range(4):
            for cb in range(4):
                tsend[k, rb * 4 + cb, 128:160, :] = block[32 * rb : 32 * rb + 32, 128 * cb : 128 * cb + 128]
        tbuf[z ^ k, plane, 128:160, :] = tsend[k, plane, 128:160, :]
        for i, (a, b) in enumerate(PLANE):
            to = (x + a) % 4 * 4 + (y + b) % 4
            push(tsend.at[k, to, pl.ds(128, 32)], tbuf.at[z ^ k, plane, pl.ds(128, 32)], gs.at[k, i], gr.at[k, i], in_plane(a, b))

    tile_wo(0, cbuf[z])
    along_z(abuf, acs, acr, 2)
    quarter(sbuf, sq, scs, scr, 0, 1)
    quarter(sbuf, sq, scs, scr, 1, 7)

    loads[7].wait()
    grad_t = nt(wob[:, 0:512], cbuf[0])
    for part in range(1, 4):
        grad_t += nt(wob[:, 512 * part : 512 * part + 512], cbuf[part])
    grad_t = grad_t.astype(BF)
    for g in range(2):
        left = jnp.concatenate([grad_t[64 * (4 * g + e) : 64 * (4 * g + e) + 64] for e in range(4)], axis=1)
        vbuf[z, 64 * g : 64 * g + 64, :] = nn(left, pst[4 * g : 4 * g + 4].reshape(4 * T, T)).astype(BF)
    along_z(vbuf, vcs, vcr, 1)
    along_z(vbuf, vcs, vcr, 3)
    quarter(sbuf, sq, scs, scr, 2, 2)
    along_z(vbuf, vcs, vcr, 2)
    tile_wv(0, sbuf[z])
    gram_in[...] = jnp.zeros_like(gram_in)

    def settle_wo(k):
        def take(src, carry):
            gram_in[pl.ds((z ^ k) * 16 + src, 128, stride=PITCH), :] = tbuf[z ^ k, src, 0:128, :].astype(F32)
            return carry

        for i, (a, b) in enumerate(PLANE):
            src = (x - a) % 4 * 4 + (y - b) % 4
            arrived(tbuf.at[z ^ k, src, pl.ds(0, 128)], hs.at[k, i], hr.at[k, i])
        lax.fori_loop(0, 16, take, 0)

    def settle_wv(k):
        def take(src, carry):
            gram_in[pl.ds(128 * PITCH + (z ^ k) * 16 + src, 32, stride=PITCH), :] = tbuf[z ^ k, src, 128:160, :].astype(F32)
            return carry

        for i, (a, b) in enumerate(PLANE):
            src = (x - a) % 4 * 4 + (y - b) % 4
            arrived(tbuf.at[z ^ k, src, pl.ds(128, 32)], gs.at[k, i], gr.at[k, i])
        lax.fori_loop(0, 16, take, 0)

    def next_wo(k):
        arrived(abuf.at[z ^ k], acs.at[k], acr.at[k])
        complete(cq, ccs, ccr, k)
        tile_wo(k, cq[z ^ k])

    def next_wv(k):
        arrived(vbuf.at[z ^ k], vcs.at[k], vcr.at[k])
        complete(sq, scs, scr, k)
        tile_wv(k, sq[z ^ k])

    relay(cq, ccs, ccr, 1)
    relay(cq, ccs, ccr, 3)
    next_wo(1)
    relay(cq, ccs, ccr, 2)
    next_wo(3)
    relay(sq, scs, scr, 1)
    relay(sq, scs, scr, 3)
    next_wv(1)
    next_wo(2)
    relay(sq, scs, scr, 2)
    next_wv(3)
    next_wv(2)
    def pair(r, u, first, size):
        at = (r * 32 + 2 * u) * PITCH + first
        upper = gram_in[pl.ds(pl.multiple_of(at, 8), size), :]
        lower = gram_in[pl.ds(pl.multiple_of(at + PITCH, 8), size), :]
        return jnp.concatenate([upper, lower], axis=1).astype(BF)

    def products(r, total):
        for u in range(16):
            both = pair(r, u, 0, 64)
            total = total + nt(both, both)
        return total

    late = (z ^ 2) * 16

    def late_products(r, total):
        for u in range(16):
            total = total + nt(pair(r, u, 0, 64), pair(r, u, late, 16))
        return total

    for k in (0, 1, 3):
        settle_wo(k)
    kd[:, 0:64] = lax.fori_loop(0, 4, products, jnp.zeros((64, 64), F32))
    settle_wv(0)
    settle_wv(1)
    settle_wo(2)
    strip = lax.fori_loop(0, 4, late_products, jnp.zeros((64, 16), F32))
    wide = jnp.concatenate([strip, jnp.zeros((64, 112), F32)], axis=1)
    wide = pltpu.roll(wide, late, 1)[:, 0:64]
    lanes = lax.broadcasted_iota(jnp.int32, (64, 64), 1)
    kd[:, 0:64] = jnp.where((lanes >= late) & (lanes < late + 16), wide, kd[:, 0:64])
    kd[pl.ds(pl.multiple_of(late, 16), 16), 0:64] = jnp.transpose(strip)
    settle_wv(3)
    settle_wv(2)
    kd[:, 0:64] = products(4, kd[:, 0:64])
    eye = lax.broadcasted_iota(jnp.int32, (64, 64), 0) == lanes
    diag = jnp.sum(jnp.where(eye, kd[:, 0:64], 0.0), axis=0, keepdims=True)
    kd[:, 64:128] = jnp.broadcast_to(diag, (64, 64))
    for g in range(16):
        fin[g] = kd[pl.ds(g, 4, stride=16), :]
    f1[plane] = fin[plane]
    for i, (a, b) in enumerate(PLANE):
        to = (x + a) % 4 * 4 + (y + b) % 4
        push(fin.at[to], f1.at[plane], f1s.at[i], f1r.at[i], in_plane(a, b))
    for i, (a, b) in enumerate(PLANE):
        src = (x - a) % 4 * 4 + (y - b) % 4
        arrived(f1.at[src], f1s.at[i], f1r.at[i])
    rows = jnp.sum(f1[...], axis=0)
    for zz in range(4):
        rowbuf[zz] = rows[zz : zz + 1]
    f2[column] = rowbuf[z]
    for i, (dw, dc) in enumerate(COLUMN):
        to = in_column(dw, dc)
        push(rowbuf.at[to[0]], f2.at[column], f2s.at[i], f2r.at[i], to)
    for i, (dw, dc) in enumerate(COLUMN):
        src = (w - dw) % 8 * 2 + (c - dc) % 2
        arrived(f2.at[src], f2s.at[i], f2r.at[i])
    total = jnp.sum(f2[...], axis=0)
    entries, diagonal = total[:, 0:64], total[:, 64:128]
    own_lane = lax.broadcasted_iota(jnp.int32, (1, 64), 1) == z * 16 + plane
    own = jnp.sum(jnp.where(own_lane, diagonal, 0.0), axis=1, keepdims=True)
    out[...] = entries / jnp.sqrt(own * diagonal)
    for copy in sent:
        copy.wait_send()


def on_device(states, cotangent, wq, wk, wv, wo):
    cos, sin = rope_tables()
    any_spec = pl.BlockSpec(memory_space=pl.ANY)
    dma = pltpu.SemaphoreType.DMA
    shapes = [
        ((2048, 512), BF), ((2048, 128), BF), ((2048, 128), BF), ((512, 2048), BF), ((T, T), F32), ((T, T), F32),
        ((4, T, 512), BF), ((4, T, 512), BF), ((4, T, 512), BF), ((4, T, 512), BF),
        ((T, 512), F32), ((T, 128), F32), ((T, 128), F32),
        ((8, T, T), BF), ((4, 512, T), BF), ((4, 128, T), BF),
        ((4, 16, 160, 128), BF), ((4, 16, 160, 128), BF),
        ((160 * PITCH, 128), F32), ((64, 128), F32), ((16, 4, 128), F32), ((16, 4, 128), F32),
        ((4, 1, 128), F32), ((16, 1, 128), F32),
    ]
    sems = [(8,)] + [(10,)] * 2 + [(4,)] * 4 + [(6,)] * 4 + [(4, 15)] * 4 + [(15,)] * 4
    return pl.pallas_call(
        kernel,
        out_shape=jax.ShapeDtypeStruct((1, 64), F32),
        in_specs=[any_spec] * 8,
        out_specs=pl.BlockSpec(memory_space=pltpu.VMEM),
        scratch_shapes=[pltpu.VMEM(s, t) for s, t in shapes] + [dma(s) for s in sems],
        compiler_params=pltpu.CompilerParams(
            collective_id=0, has_side_effects=True, vmem_limit_bytes=60 * 2**20),
        name="ntk_gram",
    )(states, cotangent, wq, wk, wv, wo, jnp.asarray(cos), jnp.asarray(sin))


def solution(mesh):
    split = Mesh(mesh.devices.reshape(4, 4, 4, 2, 2), AXES)
    seq, tp = ("z", "x", "y"), ("h", "c")
    return jax.shard_map(
        on_device,
        mesh=split,
        in_specs=(P(seq, None, tp), P(seq, None, tp), P(None, tp), P(None, tp), P(None, tp), P(tp, None)),
        out_specs=P(seq, None),
        check_vma=False,
    )
```

time: 81.3 us -> 76.3 us (0.938)
  Pallas kernels: 79.9 us -> 75.1 us
    pallas_call x1, Pallas kernels: 79.9 us -> 75.1 us  [on_device(): pl.pallas_call(kernel, out_shape=jax.ShapeDtypeStruct((1, 64), F32), in_s...]
where the time goes in v2:
time: 76.3 us
  Pallas kernels  75.1 us (98%)
  local copies, waits for them, and re-layouts  1.19 us (2%)
    pallas_call x1, Pallas kernels, on_device(): pl.pallas_call(kernel, out_shape=jax.ShapeDtypeStruct((1, 64), F32), in_s...  75.1 us

profile of v2, /device:TPU:1, one launch (start us, length us, event | category | flops | bytes accessed | tf_op | source)
XLA Modules:
  0.0 76.3 jit_solution(3905254476995004174)
XLA Ops:
  0.0 75.1 %ntk_gram.1 = f32[1,64]{1,0:T(1,128)} custom-call(bf16[1,128,512]{2,1,0:T(8,128)(2,1)} %st.1, bf16[1,128,512]{2,1,0:T(8,128)(2,1)} %ct.1, bf16[2048,512]{1,0:T(8,128)(2,1)} %wq.1, bf16[2048,128]{1,0:T(8,128)(2,1)} %wk.1, bf16[2048,128]{1,0:T(8,128)(2,1)} %wv.1, bf16[512,2048]{1,0:T(8,128)(2,1)} %wo.1, f32[128,128]{1,0:T(8,128)} %constant.4.clone.cos_in, ...), custom_call_target="tpu_custom_call" | custom-call | tf_op jit(solution)/shard_map/ntk_gram/pallas_call | solution.py:353
  75.1 1.2 %copy.10 = f32[1,64]{1,0:T(1,128)} copy(f32[1,64]{1,0:T(1,128)} %ntk_gram.1) | data formatting | bytes 512

commit v3 on v2

--- a/solution.py
+++ b/solution.py
@@ -46,7 +46,7 @@
     return v * cos + turned * sin
 
 
-def kernel(st, ct, wq, wk, wv, wo, cos_in, sin_in, out, wqb, wkb, wvb, wob, cos, sin, sbuf, cbuf, sq, cq, qacc, kacc, vacc,
+def kernel(st, ct, wq, wk, wv, wo, cos_in, sin_in, out, wqb, wkb, wvb, wob, cos, sin, sbuf, cbuf, sq, cq, qacc, kacc, vacc, gacc,
            pst, abuf, vbuf, tsend, tbuf, gram_in, kd, fin, f1, rowbuf, f2,
            loc, tps, tpr, acs, acr, vcs, vcr, ccs, ccr, scs, scr, hs, hr, gs, gr, f1s, f1r, f2s, f2r):
     z, x, y, h, c = [lax.axis_index(a) for a in AXES]
@@ -79,24 +79,39 @@
     def arrived(slot, send, recv):
         remote(slot, slot, send, recv, sibling).wait_recv()
 
-    loads = [pltpu.make_async_copy(a, b, loc.at[i]) for i, (a, b) in enumerate(
-        [(st.at[0], sbuf.at[p]), (ct.at[0], cbuf.at[p]), (wq, wqb), (wk, wkb), (wv, wvb), (cos_in, cos), (sin_in, sin), (wo, wob)])]
-    for load in loads:
-        load.start()
-
     barrier = pltpu.get_barrier_semaphore()
     for dw, dc in COLUMN:
         pl.semaphore_signal(barrier, inc=1, device_id=in_column(dw, dc), device_id_type=MESH)
     for a, b in PLANE:
         pl.semaphore_signal(barrier, inc=1, device_id=in_plane(a, b), device_id_type=MESH)
+    loads = [pltpu.make_async_copy(a, b, loc.at[i]) for i, (a, b) in enumerate(
+        [(st.at[0], sbuf.at[p]), (ct.at[0], cbuf.at[p]), (wq, wqb), (wk, wkb), (wv, wvb), (cos_in, cos), (sin_in, sin), (wo, wob)])]
+    for load in loads:
+        load.start()
     pl.semaphore_wait(barrier, len(PLANE) + len(COLUMN))
 
     halves = [pl.ds(0, 256), pl.ds(256, 256)]
 
-    def exchange(buf, base):
+    def to_opposite(buf, base):
         for i, cols in enumerate(halves):
             push(buf.at[p, :, cols], buf.at[p, :, cols], tps.at[base + i], tpr.at[base + i], opposite)
+
+    def to_sibling(buf, base):
         push(buf.at[p], buf.at[p], tps.at[base + 2], tpr.at[base + 2], sibling)
+
+    near = (h == z // 2)
+    strips = [pl.ds(0, 64), pl.ds(64, 64)]
+
+    def spread(t, which, core):
+        rows = strips[core]
+        return remote(cbuf.at[p, rows, :], cq.at[z, rows, :], ccs.at[2 * which + core], ccr.at[z], (p, x, y, t, core))
+
+    kept_here = 2 * (1 - h) + c == z
+    kept_there = 2 * (1 - h) + 1 - c == z
+
+    def cot_half(part, i, at, device):
+        cols = halves[i]
+        return remote(cbuf.at[part, :, cols], cbuf.at[part, :, cols], tps.at[at + i], tpr.at[at + i], device)
 
     def from_sibling(buf, base):
         arrived(buf.at[h * 2 + 1 - c], tps.at[base + 2], tpr.at[base + 2])
@@ -110,9 +125,18 @@
         arrived(buf.at[2 * (1 - h) + 1 - c, :, halves[i]], tps.at[base + 3 + i], tpr.at[base + 3 + i])
 
     loads[0].wait()
-    exchange(sbuf, 0)
+    to_opposite(sbuf, 0)
+    to_sibling(sbuf, 0)
     loads[1].wait()
-    exchange(cbuf, 5)
+    to_sibling(cbuf, 5)
+    for core in range(2):
+        spread(1 - h, 0, core).start()
+
+    @pl.when(z != p)
+    def _():
+        for core in range(2):
+            spread(h, 1, core).start()
+
     def project(part, i, width, first=False):
         rows = pl.ds(pl.multiple_of(part * 512 + 256 * i, 256), width)
         s = sbuf[part, :, 256 * i : 256 * i + width]
@@ -163,7 +187,22 @@
     def along_z(buf, send, recv, k):
         push(buf.at[z], buf.at[z], send.at[k], recv.at[k], (z ^ k, x, y, h, c))
 
-    along_z(abuf, acs, acr, 1)
+    inner = (z == 1) | (z == 2)
+    outer = (z == 0) | (z == 3)
+    second = jnp.where(inner, 3, 2)
+    third = jnp.where(inner, 2, 3)
+
+    def hand(slot, k, step):
+        return remote(abuf.at[z ^ slot], abuf.at[z ^ slot], acs.at[step], acr.at[slot ^ k], (z ^ k, x, y, h, c))
+
+    def attended_from(k):
+        arrived(abuf.at[z ^ k], acs.at[0], acr.at[k])
+
+    hand(0, 1, 0).start()
+
+    @pl.when(inner)
+    def _():
+        hand(0, 3, 1).start()
 
     mine = pl.ds(pl.multiple_of(64 * c, 64), 64)
     others = pl.ds(pl.multiple_of(64 * (1 - c), 64), 64)
@@ -179,15 +218,28 @@
     def complete(kept, send, recv, k):
         arrived(kept.at[z ^ k, others, :], send.at[2 + k], recv.at[2 + k])
 
+    def own_quarter():
+        return remote(cq.at[z, mine, :], cq.at[z, mine, :], ccs.at[4], ccr.at[4 + z], sibling)
+
+    def relay_wo(k):
+        zz = z ^ k
+        arrived(cq.at[zz, mine, :], ccs.at[0], ccr.at[zz])
+        push(cq.at[zz, mine, :], cq.at[zz, mine, :], ccs.at[4 + k], ccr.at[4 + zz], sibling)
+
     from_sibling(cbuf, 5)
-    from_opposite(cbuf, 5, 0)
-    from_opposite(cbuf, 5, 1)
-    forwarded(cbuf, 5, 0)
-    forwarded(cbuf, 5, 1)
-    quarter(cbuf, cq, ccs, ccr, 0, 1)
-    quarter(cbuf, cq, ccs, ccr, 1, 7)
-    quarter(cbuf, cq, ccs, ccr, 2, 6)
-    along_z(abuf, acs, acr, 3)
+
+    @pl.when(near)
+    def _():
+        cq[z] = cbuf[z]
+
+    @pl.when(jnp.logical_not(near))
+    def _():
+        arrived(cq.at[z, mine, :], ccs.at[0], ccr.at[z])
+        own_quarter().start()
+        arrived(cq.at[z, others, :], ccs.at[0], ccr.at[4 + z])
+
+    def rows_out(k, i, to, device):
+        return remote(tsend.at[k, to, pl.ds(0, 128)], tbuf.at[z ^ k, plane, pl.ds(0, 128)], hs.at[k, i], hr.at[k, i], device)
 
     def tile_wo(k, right):
         for rb in range(4):
@@ -197,7 +249,7 @@
         tbuf[z ^ k, plane, 0:128, :] = tsend[k, plane, 0:128, :]
         for i, (a, b) in enumerate(PLANE):
             to = (x + a) % 4 * 4 + (y + b) % 4
-            push(tsend.at[k, to, pl.ds(0, 128)], tbuf.at[z ^ k, plane, pl.ds(0, 128)], hs.at[k, i], hr.at[k, i], in_plane(a, b))
+            rows_out(k, i, to, in_plane(a, b)).start()
 
     def tile_wv(k, right):
         block = nn(vbuf[z ^ k], right).astype(BF)
@@ -209,24 +261,7 @@
             to = (x + a) % 4 * 4 + (y + b) % 4
             push(tsend.at[k, to, pl.ds(128, 32)], tbuf.at[z ^ k, plane, pl.ds(128, 32)], gs.at[k, i], gr.at[k, i], in_plane(a, b))
 
-    tile_wo(0, cbuf[z])
-    along_z(abuf, acs, acr, 2)
-    quarter(sbuf, sq, scs, scr, 0, 1)
-    quarter(sbuf, sq, scs, scr, 1, 7)
-
-    loads[7].wait()
-    grad_t = nt(wob[:, 0:512], cbuf[0])
-    for part in range(1, 4):
-        grad_t += nt(wob[:, 512 * part : 512 * part + 512], cbuf[part])
-    grad_t = grad_t.astype(BF)
-    for g in range(2):
-        left = jnp.concatenate([grad_t[64 * (4 * g + e) : 64 * (4 * g + e) + 64] for e in range(4)], axis=1)
-        vbuf[z, 64 * g : 64 * g + 64, :] = nn(left, pst[4 * g : 4 * g + 4].reshape(4 * T, T)).astype(BF)
-    along_z(vbuf, vcs, vcr, 1)
-    along_z(vbuf, vcs, vcr, 3)
-    quarter(sbuf, sq, scs, scr, 2, 2)
-    along_z(vbuf, vcs, vcr, 2)
-    tile_wv(0, sbuf[z])
+    tile_wo(0, cq[z])
     gram_in[...] = jnp.zeros_like(gram_in)
 
     def settle_wo(k):
@@ -250,27 +285,97 @@
         lax.fori_loop(0, 16, take, 0)
 
     def next_wo(k):
-        arrived(abuf.at[z ^ k], acs.at[k], acr.at[k])
-        complete(cq, ccs, ccr, k)
-        tile_wo(k, cq[z ^ k])
+        zz = z ^ k
+        arrived(cq.at[zz, others, :], ccs.at[0], ccr.at[4 + zz])
+        tile_wo(k, cq[zz])
 
     def next_wv(k):
         arrived(vbuf.at[z ^ k], vcs.at[k], vcr.at[k])
         complete(sq, scs, scr, k)
         tile_wv(k, sq[z ^ k])
 
-    relay(cq, ccs, ccr, 1)
-    relay(cq, ccs, ccr, 3)
+    attended_from(1)
+
+    @pl.when(inner)
+    def _():
+        hand(1, 3, 2).start()
+        attended_from(3)
+        hand(3, 1, 3).start()
+
+    @pl.when(p != z)
+    def _():
+        cot_half(p, 0, 5, opposite).start()
+
+    relay_wo(1)
     next_wo(1)
-    relay(cq, ccs, ccr, 2)
-    next_wo(3)
+    relay_wo(3)
+    relay_wo(2)
+
+    @pl.when(inner)
+    def _():
+        attended_from(2)
+        hand(2, 1, 4).start()
+
+    @pl.when(outer)
+    def _():
+        attended_from(2)
+
+    @pl.when(p != z)
+    def _():
+        cot_half(p, 1, 5, opposite).start()
+
+    next_wo(second)
+    @pl.when(outer)
+    def _():
+        attended_from(3)
+
+    next_wo(third)
+
+    def grad_part(part):
+        cols = pl.ds(pl.multiple_of(part * 512, 512), 512)
+        return nt(wob[:, cols], cbuf[part])
+
+    loads[7].wait()
+    gacc[...] = grad_part(p) + grad_part(h * 2 + 1 - c)
+
+    @pl.when(jnp.logical_not(kept_here))
+    def _():
+        for i in range(2):
+            cot_half(2 * (1 - h) + c, i, 5, opposite).wait_recv()
+            cot_half(2 * (1 - h) + c, i, 8, sibling).start()
+
+    @pl.when(kept_here)
+    def _():
+        cbuf[2 * (1 - h) + c] = cq[z]
+
+    quarter(sbuf, sq, scs, scr, 0, 1)
+    quarter(sbuf, sq, scs, scr, 1, 7)
+    quarter(sbuf, sq, scs, scr, 2, 2)
+    gacc[...] = gacc[...] + grad_part(2 * (1 - h) + c)
+
+    @pl.when(jnp.logical_not(kept_there))
+    def _():
+        for i in range(2):
+            cot_half(2 * (1 - h) + 1 - c, i, 8, sibling).wait_recv()
+
+    @pl.when(kept_there)
+    def _():
+        cbuf[2 * (1 - h) + 1 - c] = cq[z]
+
+    gacc[...] = gacc[...] + grad_part(2 * (1 - h) + 1 - c)
+    for g in range(2):
+        left = jnp.concatenate([gacc[64 * (4 * g + e) : 64 * (4 * g + e) + 64, :] for e in range(4)], axis=1).astype(BF)
+        vbuf[z, 64 * g : 64 * g + 64, :] = nn(left, pst[4 * g : 4 * g + 4].reshape(4 * T, T)).astype(BF)
+    along_z(vbuf, vcs, vcr, 1)
+    along_z(vbuf, vcs, vcr, 3)
+    along_z(vbuf, vcs, vcr, 2)
+    tile_wv(0, sbuf[z])
     relay(sq, scs, scr, 1)
     relay(sq, scs, scr, 3)
-    next_wv(1)
-    next_wo(2)
     relay(sq, scs, scr, 2)
-    next_wv(3)
-    next_wv(2)
+    for k in (1, 3, 2):
+        next_wv(k)
+
     def pair(r, u, first, size):
         at = (r * 32 + 2 * u) * PITCH + first
         upper = gram_in[pl.ds(pl.multiple_of(at, 8), size), :]
@@ -283,19 +388,19 @@
             total = total + nt(both, both)
         return total
 
-    late = (z ^ 2) * 16
+    late = (z ^ third) * 16
 
     def late_products(r, total):
         for u in range(16):
             total = total + nt(pair(r, u, 0, 64), pair(r, u, late, 16))
         return total
 
-    for k in (0, 1, 3):
+    for k in (0, 1, second):
         settle_wo(k)
     kd[:, 0:64] = lax.fori_loop(0, 4, products, jnp.zeros((64, 64), F32))
     settle_wv(0)
     settle_wv(1)
-    settle_wo(2)
+    settle_wo(third)
     strip = lax.fori_loop(0, 4, late_products, jnp.zeros((64, 16), F32))
     wide = jnp.concatenate([strip, jnp.zeros((64, 112), F32)], axis=1)
     wide = pltpu.roll(wide, late, 1)[:, 0:64]
@@ -334,6 +439,37 @@
     out[...] = entries / jnp.sqrt(own * diagonal)
     for copy in sent:
         copy.wait_send()
+    for k in range(4):
+        for i, (a, b) in enumerate(PLANE):
+            rows_out(k, i, 0, in_plane(a, b)).wait_send()
+
+    @pl.when(p != z)
+    def _():
+        for i in range(2):
+            cot_half(p, i, 5, opposite).wait_send()
+
+    @pl.when(jnp.logical_not(kept_here))
+    def _():
+        for i in range(2):
+            cot_half(p, i, 8, sibling).wait_send()
+
+    hand(0, 1, 0).wait_send()
+    for core in range(2):
+        spread(1 - h, 0, core).wait_send()
+
+    @pl.when(z != p)
+    def _():
+        for core in range(2):
+            spread(h, 1, core).wait_send()
+
+    @pl.when(jnp.logical_not(near))
+    def _():
+        own_quarter().wait_send()
+
+    @pl.when(inner)
+    def _():
+        for step in range(1, 5):
+            hand(0, 1, step).wait_send()
 
 
 def on_device(states, cotangent, wq, wk, wv, wo):
@@ -343,13 +479,13 @@
     shapes = [
         ((2048, 512), BF), ((2048, 128), BF), ((2048, 128), BF), ((512, 2048), BF), ((T, T), F32), ((T, T), F32),
         ((4, T, 512), BF), ((4, T, 512), BF), ((4, T, 512), BF), ((4, T, 512), BF),
-        ((T, 512), F32), ((T, 128), F32), ((T, 128), F32),
+        ((T, 512), F32), ((T, 128), F32), ((T, 128), F32), ((512, T), F32),
         ((8, T, T), BF), ((4, 512, T), BF), ((4, 128, T), BF),
         ((4, 16, 160, 128), BF), ((4, 16, 160, 128), BF),
         ((160 * PITCH, 128), F32), ((64, 128), F32), ((16, 4, 128), F32), ((16, 4, 128), F32),
         ((4, 1, 128), F32), ((16, 1, 128), F32),
     ]
-    sems = [(8,)] + [(10,)] * 2 + [(4,)] * 4 + [(6,)] * 4 + [(4, 15)] * 4 + [(15,)] * 4
+    sems = [(8,)] + [(10,)] * 2 + [(5,)] * 4 + [(8,)] * 4 + [(4, 15)] * 4 + [(15,)] * 4
     return pl.pallas_call(
         kernel,
         out_shape=jax.ShapeDtypeStruct((1, 64), F32),

time: 76.3 us -> 72.2 us (0.946)
  Pallas kernels: 75.1 us -> 70.9 us
    pallas_call x1, Pallas kernels: 75.1 us -> 70.9 us  [on_device(): pl.pallas_call(kernel, out_shape=jax.ShapeDtypeStruct((1, 64), F32), in_s...]
where the time goes in v3:
time: 72.2 us; the launch traced here: 72.1 us
  Pallas kernels  70.9 us (98%)
  local copies, waits for them, and re-layouts  1.19 us (2%)
    pallas_call x1, Pallas kernels, on_device(): pl.pallas_call(kernel, out_shape=jax.ShapeDtypeStruct((1, 64), F32), in_s...  70.9 us

profile of v3, /device:TPU:1, one launch (start us, length us, event | category | flops | bytes accessed | tf_op | source)
XLA Modules:
  0.0 72.1 jit_solution(9458330065699862909)
XLA Ops:
  0.0 70.9 %ntk_gram.1 = f32[1,64]{1,0:T(1,128)} custom-call(bf16[1,128,512]{2,1,0:T(8,128)(2,1)} %st.1, bf16[1,128,512]{2,1,0:T(8,128)(2,1)} %ct.1, bf16[2048,512]{1,0:T(8,128)(2,1)} %wq.1, bf16[2048,128]{1,0:T(8,128)(2,1)} %wk.1, bf16[2048,128]{1,0:T(8,128)(2,1)} %wv.1, bf16[512,2048]{1,0:T(8,128)(2,1)} %wo.1, f32[128,128]{1,0:T(8,128)} %constant.4.clone.cos_in, ...), custom_call_target="tpu_custom_call" | custom-call | tf_op jit(solution)/shard_map/ntk_gram/pallas_call | solution.py:489
  70.9 1.2 %copy.10 = f32[1,64]{1,0:T(1,128)} copy(f32[1,64]{1,0:T(1,128)} %ntk_gram.1) | data formatting | bytes 512

commit v4 on v3

--- a/solution.py
+++ b/solution.py
@@ -436,7 +436,8 @@
     entries, diagonal = total[:, 0:64], total[:, 64:128]
     own_lane = lax.broadcasted_iota(jnp.int32, (1, 64), 1) == z * 16 + plane
     own = jnp.sum(jnp.where(own_lane, diagonal, 0.0), axis=1, keepdims=True)
-    out[...] = entries / jnp.sqrt(own * diagonal)
+    out[0:1, :] = entries
+    out[1:2, :] = own * diagonal
     for copy in sent:
         copy.wait_send()
     for k in range(4):
@@ -486,9 +487,9 @@
         ((4, 1, 128), F32), ((16, 1, 128), F32),
     ]
     sems = [(8,)] + [(10,)] * 2 + [(5,)] * 4 + [(8,)] * 4 + [(4, 15)] * 4 + [(15,)] * 4
-    return pl.pallas_call(
+    both = pl.pallas_call(
         kernel,
-        out_shape=jax.ShapeDtypeStruct((1, 64), F32),
+        out_shape=jax.ShapeDtypeStruct((2, 64), F32),
         in_specs=[any_spec] * 8,
         out_specs=pl.BlockSpec(memory_space=pltpu.VMEM),
         scratch_shapes=[pltpu.VMEM(s, t) for s, t in shapes] + [dma(s) for s in sems],
@@ -496,6 +497,7 @@
             collective_id=0, has_side_effects=True, vmem_limit_bytes=60 * 2**20),
         name="ntk_gram",
     )(states, cotangent, wq, wk, wv, wo, jnp.asarray(cos), jnp.asarray(sin))
+    return both[0:1] / jnp.sqrt(both[1:2])
 
 
 def solution(mesh):

time: 72.2 us -> 72.3 us (level)
  other arithmetic: 0 us -> 1.28 us
  local copies, waits for them, and re-layouts: 1.19 us -> 0 us
    div x0 -> x1, other arithmetic: none -> 1.28 us  [on_device(): return both[0:1] / jnp.sqrt(both[1:2])]
    unnamed x1 -> x0, local copies, waits for them, and re-layouts: 1.19 us -> none
where the time goes in v4:
time: 72.3 us; the launch traced here: 72.2 us
  Pallas kernels  70.9 us (98%)
  other arithmetic  1.28 us (2%)
    pallas_call x1, Pallas kernels, on_device(): pl.pallas_call(kernel, out_shape=jax.ShapeDtypeStruct((2, 64), F32), in_s...  70.9 us

profile of v4, /device:TPU:1, one launch (start us, length us, event | category | flops | bytes accessed | tf_op | source)
XLA Modules:
  0.0 72.2 jit_solution(12630150073943024591)
XLA Ops:
  0.0 70.9 %ntk_gram.1 = f32[2,64]{1,0:T(2,128)} custom-call(bf16[1,128,512]{2,1,0:T(8,128)(2,1)} %st.1, bf16[1,128,512]{2,1,0:T(8,128)(2,1)} %ct.1, bf16[2048,512]{1,0:T(8,128)(2,1)} %wq.1, bf16[2048,128]{1,0:T(8,128)(2,1)} %wk.1, bf16[2048,128]{1,0:T(8,128)(2,1)} %wv.1, bf16[512,2048]{1,0:T(8,128)(2,1)} %wo.1, f32[128,128]{1,0:T(8,128)} %constant.4.clone.cos_in, ...), custom_call_target="tpu_custom_call" | custom-call | tf_op jit(solution)/shard_map/ntk_gram/pallas_call | solution.py:490
  70.9 1.3 %rsqrt_multiply_fusion = f32[1,64]{1,0:T(1,128)} fusion(f32[2,64]{1,0:T(2,128)} %ntk_gram.1), kind=kLoop, calls=%fused_computation | loop fusion | flops 64 | bytes 768 | tf_op jit(solution)/shard_map/div | solution.py:500
